TPU v7x, 32 devices: a whole 2x2x4 slice. The times are simulated.
32 devices in a mesh: dp: 8 (over y, x, core), branch: 4 (over z).
Axes of the slice: x: 2, y: 2, z: 4, core: 2. Of those that a mesh axis runs over, the one named last changes fastest.
Arguments:
- image_hidden: bfloat16 [4096, 1024], P('dp', 'branch'), may hold values from -8 to 8
- text_hidden: bfloat16 [4096, 768], P('dp', 'branch'), may hold values from -8 to 8
- image_proj: bfloat16 [1024, 768], replicated, may hold values from -0.1875 to 0.1875
- text_proj: bfloat16 [768, 768], replicated, may hold values from -0.21650635 to 0.21650635
- log_inverse_sharpness: float32 [1], replicated, may hold values from 4 to 5.9
- partner: int32 [4096], replicated, may hold values from 0 to 4095, each once
Outputs:
- loss: float32 [1], replicated
- grad_log_scale: float32 [1], replicated
- grad_image_hidden: bfloat16 [4096, 1024], P('dp', 'branch')
- grad_text_hidden: bfloat16 [4096, 768], P('dp', 'branch')
- grad_image_proj: float32 [1024, 768], P('branch')
- grad_text_proj: float32 [768, 768], P('branch')
Inputs may be any that keep to these rules, and one draw needn't show every extreme that they name: `partner`: each text index appears exactly once.
All inputs are finite; a program needn't handle non-finite values.
Results may differ from a plain program's by a relative error of at most 0.0029.
The roundings to bfloat16 on the way count: a program that leaves them out, or rounds other values in their place, can miss the bound.
Values may be sent and summed in bfloat16 or wider, within the bound.
A program may use at most 64 MiB of HBM per device.

v0:
```python
import jax
import jax.numpy as jnp
from jax import lax
from jax.sharding import PartitionSpec as P

NORM_EPSILON = 1e-06


def normalize(raw_rows):
    lengths = jnp.sqrt(jnp.sum(raw_rows * raw_rows, axis=1, keepdims=True) + NORM_EPSILON)
    unit_rows = raw_rows / lengths
    return (unit_rows, lengths, unit_rows.astype(jnp.bfloat16))


def unnormalize(upstream, unit_rows, lengths):
    radial = jnp.sum(upstream * unit_rows, axis=1, keepdims=True)
    return ((upstream - unit_rows * radial) / lengths).astype(jnp.bfloat16)


def per_device(image_hidden, text_hidden, image_proj, text_proj, log_inverse_sharpness, partner):
    branch_count = lax.axis_size("branch")
    data_count = lax.axis_size("dp")
    branch_pos = lax.axis_index("branch")
    data_pos = lax.axis_index("dp")
    group_rows = image_hidden.shape[0]
    own_rows = group_rows // branch_count
    image_cols = image_hidden.shape[1]
    text_cols = text_hidden.shape[1]
    image_slab = lax.dynamic_slice_in_dim(image_proj, branch_pos * image_cols, image_cols, 0)
    text_slab = lax.dynamic_slice_in_dim(text_proj, branch_pos * text_cols, text_cols, 0)
    image_local, text_local = (
        lax.all_to_all(image_hidden, "branch", split_axis=0, concat_axis=1, tiled=True),
        lax.all_to_all(text_hidden, "branch", split_axis=0, concat_axis=1, tiled=True),
    )
    image_raw = jnp.dot(image_local, image_proj, preferred_element_type=jnp.float32)
    text_raw = jnp.dot(text_local, text_proj, preferred_element_type=jnp.float32)
    image_unit, image_length, image_emb = normalize(image_raw)
    text_unit, text_length, caption_feature_entries = normalize(text_raw)
    normalized_exponent_divisor = jnp.exp(log_inverse_sharpness[0])
    column_count = own_rows * data_count
    total_pairs = group_rows * data_count
    denominator = 2.0 * total_pairs
    group_emb = lax.all_gather(image_emb, "branch", axis=0, tiled=True)
    row_partner = lax.dynamic_slice_in_dim(partner, data_pos * group_rows, group_rows, 0)

    def column_ident(positions):
        return (positions // own_rows * branch_count + branch_pos) * own_rows + positions % own_rows

    block_piece = lax.all_gather(caption_feature_entries, "dp", axis=0, tiled=True)
    row_peak = jnp.full((group_rows,), -jnp.inf, jnp.float32)
    row_mass = jnp.zeros((group_rows,), jnp.float32)
    piece_width = block_piece.shape[0]
    matching_cosine_scores = normalized_exponent_divisor * lax.dot_general(
        group_emb, block_piece, (((1,), (1,)), ((), ())), preferred_element_type=jnp.float32
    )
    logits_kept = matching_cosine_scores
    column_ids = column_ident(jnp.arange(piece_width, dtype=jnp.int32))
    matched = row_partner[:, None] == column_ids[None, :]
    positive = jnp.sum(jnp.where(matched, matching_cosine_scores, 0.0), axis=1)
    new_peak = jnp.max(matching_cosine_scores, axis=1)
    row_mass = row_mass * jnp.exp(row_peak - new_peak) + jnp.sum(
        jnp.exp(matching_cosine_scores - new_peak[:, None]), axis=1
    )
    piece_peak = jnp.max(matching_cosine_scores, axis=0)
    piece_mass = jnp.sum(jnp.exp(matching_cosine_scores - piece_peak[None, :]), axis=0)
    column_peak = piece_peak
    column_mass = piece_mass
    (
        retained_text_rows,
        matching_cosine_scores,
        row_peak,
        row_mass,
        positive,
        column_peak,
        column_mass,
    ) = (block_piece, logits_kept, new_peak, row_mass, positive, column_peak, column_mass)
    row_highest = lax.pmax(row_peak, "branch")
    row_mass, positive = lax.psum((row_mass * jnp.exp(row_peak - row_highest), positive), "branch")
    row_peak = row_highest
    column_highest = lax.pmax(column_peak, "dp")
    column_mass = lax.psum(column_mass * jnp.exp(column_peak - column_highest), "dp")
    column_peak = column_highest
    row_lse = row_peak + jnp.log(row_mass)
    col_lse = column_peak + jnp.log(column_mass)
    column_ids = column_ident(jnp.arange(column_count, dtype=jnp.int32))
    matched = (row_partner[:, None] == column_ids[None, :]).astype(jnp.float32)
    weights = (
        jnp.exp(matching_cosine_scores - row_lse[:, None])
        + jnp.exp(matching_cosine_scores - col_lse[None, :])
        - 2.0 * matched
    ) / denominator
    scale_part = jnp.sum(weights * matching_cosine_scores)
    reduced_width_parameters = weights.astype(jnp.bfloat16)
    picture_projection_matrix = lax.psum_scatter(
        normalized_exponent_divisor
        * jnp.dot(reduced_width_parameters, retained_text_rows, preferred_element_type=jnp.float32),
        "branch",
        scatter_dimension=0,
        tiled=True,
    )
    text_up = lax.psum_scatter(
        normalized_exponent_divisor
        * lax.dot_general(
            reduced_width_parameters,
            group_emb,
            (((0,), (0,)), ((), ())),
            preferred_element_type=jnp.float32,
        ),
        "dp",
        scatter_dimension=0,
        tiled=True,
    )
    image_down = unnormalize(picture_projection_matrix, image_unit, image_length)
    text_down = unnormalize(text_up, text_unit, text_length)
    image_gathered, text_gathered = (
        lax.all_gather(image_down, "branch", axis=0, tiled=True),
        lax.all_gather(text_down, "branch", axis=0, tiled=True),
    )
    grad_image_hidden = jnp.dot(
        image_gathered, image_slab.T, preferred_element_type=jnp.float32
    ).astype(jnp.bfloat16)
    grad_text_hidden = jnp.dot(
        text_gathered, text_slab.T, preferred_element_type=jnp.float32
    ).astype(jnp.bfloat16)
    image_weight = lax.dot_general(
        image_hidden, image_gathered, (((0,), (0,)), ((), ())), preferred_element_type=jnp.float32
    )
    text_weight = lax.dot_general(
        text_hidden, text_gathered, (((0,), (0,)), ((), ())), preferred_element_type=jnp.float32
    )
    grad_image_proj, grad_text_proj = lax.psum((image_weight, text_weight), "dp")
    own_row_terms = lax.dynamic_slice_in_dim(
        row_lse - 2.0 * positive, branch_pos * own_rows, own_rows, 0
    )
    own_col_terms = lax.dynamic_slice_in_dim(col_lse, data_pos * own_rows, own_rows, 0)
    loss_part = (jnp.sum(own_row_terms) + jnp.sum(own_col_terms)) / denominator
    loss_total, scale_total = lax.psum((loss_part, scale_part), ("dp", "branch"))
    return (
        loss_total.reshape(1),
        scale_total.reshape(1),
        grad_image_hidden,
        grad_text_hidden,
        grad_image_proj,
        grad_text_proj,
    )


def solution(mesh):
    placed = (P("dp", "branch"), P("dp", "branch"), P(), P(), P(), P())
    return jax.shard_map(
        per_device,
        mesh=mesh,
        in_specs=placed,
        out_specs=(
            P(),
            P(),
            P("dp", "branch"),
            P("dp", "branch"),
            P("branch", None),
            P("branch", None),
        ),
        check_vma=False,
    )
```

profile of v0, /device:TPU:0, one launch (start us, length us, event | category | flops | bytes accessed | tf_op | source)
XLA Modules:
  0.0 283.1 jit_solution(11487178637805667783)
XLA Ops:
  7.2 0.0 copy-start
  7.2 0.0 all-gather.2.cloned.1.call-start
  7.2 1.1 copy_bitcast_fusion
  8.3 13.6 %all_to_all.38 = bf16[4,128,192]{1,2,0:T(8,128)(2,1)S(1)} all-to-all(bf16[4,128,192]{1,2,0:T(8,128)(2,1)S(1)} %copy_bitcast_fusion), channel_id=1, replica_groups=mesh['dp'=8,'branch'=4] {'branch'}, dimensions={0} | all-to-all | bytes 393216 | tf_op jit(solution)/shard_map/all_to_all | solution.py:33
  21.9 1.7 multiply_reduce_fusion.3
  23.7 0.8 fusion.20
  24.4 0.0 all-gather.2.cloned.1.call-update
  24.5 3.4 %all-to-all-start = ((bf16[4,128,256]{2,1,0:T(8,128)(2,1)}), bf16[4,128,256]{2,1,0:T(8,128)(2,1)S(1)}, u32[]{:S(2)}, u32[]{:S(2)}) async-start(bf16[4,128,256]{2,1,0:T(8,128)(2,1)} %bitcast.1), calls=%async_computation | async-start | bytes 524288 | tf_op jit(solution)/shard_map/all_to_all | solution.py:32
  27.9 0.0 reduce-scatter.3.cloned.1.call-start
  28.6 0.8 dynamic_slice.15
  29.4 6.6 %all-to-all-done = bf16[4,128,256]{2,1,0:T(8,128)(2,1)S(1)} async-done(((bf16[4,128,256]{2,1,0:T(8,128)(2,1)}), bf16[4,128,256]{2,1,0:T(8,128)(2,1)S(1)}, u32[]{:S(2)}, u32[]{:S(2)}) %all-to-all-start) | async-done | bytes 262176 | tf_op jit(solution)/shard_map/all_to_all | solution.py:32
  36.0 0.2 copy.17
  36.2 0.5 multiply_reduce_fusion.4
  36.7 0.1 fusion.19
  36.8 17.6 %all_gather.12 = bf16[512,768]{1,0:T(8,128)(2,1)S(1)} all-gather(bf16[128,768]{1,0:T(8,128)(2,1)S(1)} %fusion.19), channel_id=1, replica_groups=mesh['dp'=8,'branch'=4] {'branch'}, dimensions={0}, use_global_device_ids=true | all-gather | bytes 983040 | tf_op jit(solution)/shard_map/all_gather | solution.py:43
  54.4 3.8 %fusion.23 = (f32[1024]{0:T(1024)S(1)}, f32[512]{0:T(512)S(1)}, f32[512,1024]{1,0:T(8,128)}) fusion(bf16[512,768]{1,0:T(8,128)(2,1)S(1)} %all_gather.12, bf16[1024,768]{1,0:T(8,128)(2,1)} %all-gather.2.cloned.1.call-done, f32[]{:T(128)} %bitcast), kind=kOutput, calls=%fused_computation.55 | convolution fusion | flops 806877696 | bytes 4462596 | tf_op jit(solution)/shard_map/dot_general | solution.py:53
  58.2 10.3 %pmax.14 = f32[512]{0:T(512)S(1)} all-reduce(f32[512]{0:T(512)S(1)} %get-tuple-element.35), channel_id=1, replica_groups=mesh['dp'=8,'branch'=4] {'branch'}, use_global_device_ids=true, to_apply=%region_3.4 | all-reduce | flops 512 | bytes 4096 | tf_op jit(solution)/shard_map/pmax | solution.py:77
  68.5 11.8 %pmax.15 = f32[1024]{0:T(1024)S(1)} all-reduce(f32[1024]{0:T(1024)S(1)} %get-tuple-element.34), channel_id=1, replica_groups=mesh['dp'=8,'branch'=4] {'dp'}, use_global_device_ids=true, to_apply=%region_10.11 | all-reduce | flops 1024 | bytes 8192 | tf_op jit(solution)/shard_map/pmax | solution.py:80
  80.3 2.3 exponential_reduce_fusion
  82.7 11.9 %psum.51 = f32[1024]{0:T(1024)S(1)} all-reduce(f32[1024]{0:T(1024)S(1)} %exponential_multiply_fusion), channel_id=1, replica_groups=mesh['dp'=8,'branch'=4] {'dp'}, use_global_device_ids=true, to_apply=%region_12.13 | all-reduce | flops 1024 | bytes 8192 | tf_op jit(solution)/shard_map/psum | solution.py:81
  94.6 8.4 %psum.49 = f32[512]{0:T(512)S(1)} all-reduce(f32[512]{0:T(512)S(1)} %exponential_multiply_fusion.1), channel_id=1, replica_groups=mesh['dp'=8,'branch'=4] {'branch'}, use_global_device_ids=true, to_apply=%region_5.6 | all-reduce | flops 512 | bytes 4096 | tf_op jit(solution)/shard_map/psum | solution.py:78
  103.0 4.8 %convolution_multiply_fusion.2 = f32[512,768]{1,0:T(8,128)} fusion(bf16[1024,768]{1,0:T(8,128)(2,1)} %all-gather.2.cloned.1.call-done, f32[]{:T(128)} %bitcast, f32[512,1024]{1,0:T(8,128)} %get-tuple-element.44, f32[1024]{0:T(1024)S(1)} %log_add_fusion, f32[512]{0:T(512)S(1)} %log_add_fusion.1, s32[1024]{0:T(1024)S(1)} %fusion.15, s32[512]{0:T(512)S(1)} %dynamic_slice.15), kind=kOutput, calls=%fused_computation.11 | convolution fusion | flops 809893888 | bytes 5255172 | tf_op jit(solution)/shard_map/dot_general | solution.py:96
  107.8 0.0 reduce-scatter.3.cloned.1.call-update
  107.8 0.0 reduce-scatter.5.cloned.1.call-start
  107.9 4.8 %convolution_multiply_fusion = f32[1024,768]{1,0:T(8,128)} fusion(bf16[512,768]{1,0:T(8,128)(2,1)S(1)} %all_gather.12, f32[]{:T(128)} %bitcast, f32[512,1024]{1,0:T(8,128)} %get-tuple-element.44, f32[1024]{0:T(1024)S(1)} %log_add_fusion, f32[512]{0:T(512)S(1)} %log_add_fusion.1, s32[1024]{0:T(1024)S(1)} %fusion.15, s32[512]{0:T(512)S(1)} %dynamic_slice.15), kind=kOutput, calls=%fused_computation.9 | convolution fusion | flops 810287104 | bytes 6041604 | tf_op jit(solution)/shard_map/dot_general | solution.py:103
  112.7 0.0 reduce-scatter.5.cloned.1.call-update
  112.8 0.0 all-reduce.4.cloned.1.call-start
  112.8 0.7 dynamic-slice_reduce_fusion
  113.5 3.6 %multiply_reduce_fusion = (f32[]{:T(128)}, f32[512]{0:T(512)S(1)}) fusion(f32[512,1024]{1,0:T(8,128)} %get-tuple-element.44, f32[1024]{0:T(1024)S(1)} %log_add_fusion, f32[512]{0:T(512)S(1)} %log_add_fusion.1, s32[1024]{0:T(1024)S(1)} %fusion.15, s32[512]{0:T(512)S(1)} %dynamic_slice.15), kind=kLoop, calls=%fused_computation.5 | loop fusion | flops 5766655 | bytes 2111492 | tf_op jit(solution)/shard_map/reduce_sum | solution.py:92
  117.1 11.2 %psum.50 = f32[512]{0:T(512)S(1)} all-reduce(f32[512]{0:T(512)S(1)} %get-tuple-element.31), channel_id=1, replica_groups=mesh['dp'=8,'branch'=4] {'branch'}, use_global_device_ids=true, to_apply=%region_7.8 | all-reduce | flops 512 | bytes 4096 | tf_op jit(solution)/shard_map/psum | solution.py:78
  128.3 14.0 %reduce-scatter.3.cloned.1.call-done = f32[128,768]{1,0:T(8,128)} async-done(((f32[512,768]{1,0:T(8,128)}), f32[128,768]{1,0:T(8,128)}) %reduce-scatter.3.cloned.1.call-update) | async-done | bytes 393232 | tf_op jit(solution)/shard_map/reduce_scatter | solution.py:94
  142.3 1.2 multiply_reduce_fusion.2
  143.5 1.1 divide_convert_fusion.1
  144.6 17.9 %all_gather.14 = bf16[512,768]{1,0:T(8,128)(2,1)S(1)} all-gather(bf16[128,768]{1,0:T(8,128)(2,1)S(1)} %divide_convert_fusion.1), channel_id=1, replica_groups=mesh['dp'=8,'branch'=4] {'branch'}, dimensions={0}, use_global_device_ids=true | all-gather | bytes 983040 | tf_op jit(solution)/shard_map/all_gather | solution.py:116
  162.5 2.2 convolution_bitcast_fusion
  164.8 25.9 %reduce-scatter.5.cloned.1.call-done = f32[128,768]{1,0:T(8,128)} async-done(((f32[1024,768]{1,0:T(8,128)}), f32[128,768]{1,0:T(8,128)}) %reduce-scatter.5.cloned.1.call-update) | async-done | bytes 393232 | tf_op jit(solution)/shard_map/reduce_scatter | solution.py:101
  190.7 1.2 multiply_reduce_fusion.1
  191.8 1.1 divide_convert_fusion
  193.0 19.6 %all_gather.15 = bf16[512,768]{1,0:T(8,128)(2,1)S(1)} all-gather(bf16[128,768]{1,0:T(8,128)(2,1)S(1)} %divide_convert_fusion), channel_id=1, replica_groups=mesh['dp'=8,'branch'=4] {'branch'}, dimensions={0}, use_global_device_ids=true | all-gather | bytes 983040 | tf_op jit(solution)/shard_map/all_gather | solution.py:117
  212.5 2.1 convolution_bitcast_fusion.1
  214.6 0.0 all-reduce.4.cloned.1.call-update
  214.6 0.7 dynamic-slice_reduce_fusion.1
  216.6 38.5 %all-reduce = (f32[1]{0:T(128)}, f32[1]{0:T(128)}) all-reduce(f32[1]{0:T(128)} %bitcast.6, f32[1]{0:T(128)} %bitcast.7), channel_id=1, replica_groups=mesh['dp'=8,'branch'=4] {'dp','branch'}, use_global_device_ids=true, to_apply=%region_14.15 | all-reduce | flops 2 | bytes 16 | tf_op jit(solution)/shard_map/psum | solution.py:137
  255.1 1.1 convolution_convert_fusion
  256.2 2.0 convolution_convert_fusion.1
  258.3 14.1 %all-reduce.4.cloned.1.call-done = (f32[256,768]{0,1:T(8,128)}, f32[192,768]{1,0:T(8,128)}) async-done(((f32[256,768]{0,1:T(8,128)}, f32[192,768]{1,0:T(8,128)}), (f32[256,768]{0,1:T(8,128)}, f32[192,768]{1,0:T(8,128)})) %all-reduce.4.cloned.1.call-update) | async-done | bytes 1376272 | tf_op jit(solution)/shard_map/psum | solution.py:131
  272.3 2.3 copy.19
  274.6 1.9 copy.25
  (10 shorter events, 0.1 us)
Async XLA Ops:
  7.2 29.0 %copy-start = (bf16[1024,768]{1,0:T(8,128)(2,1)S(1)}, bf16[1024,768]{1,0:T(8,128)(2,1)}, u32[]{:S(2)}) copy-start(bf16[1024,768]{1,0:T(8,128)(2,1)} %param.8) | copy-start | bytes 4718596
  7.2 47.2 %all-gather.2.cloned.1.call-start = ((), (), s32[]{:S(2)}) async-start(), calls=%async_computation.4 | async-start | bytes 1769472 | tf_op jit(solution)/shard_map/all_gather | solution.py:49
  24.5 11.6 %all-to-all-start = ((bf16[4,128,256]{2,1,0:T(8,128)(2,1)}), bf16[4,128,256]{2,1,0:T(8,128)(2,1)S(1)}, u32[]{:S(2)}, u32[]{:S(2)}) async-start(bf16[4,128,256]{2,1,0:T(8,128)(2,1)} %bitcast.1), calls=%async_computation | async-start | bytes 524288 | tf_op jit(solution)/shard_map/all_to_all | solution.py:32
  27.9 114.4 %reduce-scatter.3.cloned.1.call-start = ((), (), s32[]{:S(2)}) async-start(), calls=%async_computation.5 | async-start | bytes 1966080 | tf_op jit(solution)/shard_map/reduce_scatter | solution.py:94
  107.8 82.8 %reduce-scatter.5.cloned.1.call-start = ((), (), s32[]{:S(2)}) async-start(), calls=%async_computation.6 | async-start | bytes 3538944 | tf_op jit(solution)/shard_map/reduce_scatter | solution.py:101
  112.8 159.6 %all-reduce.4.cloned.1.call-start = ((), (), s32[]{:S(2)}) async-start(), calls=%async_computation.7 | async-start | bytes 2752512 | tf_op jit(solution)/shard_map/psum | solution.py:131
Sparse Core Ops, SparseCore 0:
  24.6 24.6 all-gather.1
  108.0 34.2 reduce-scatter.2
  145.7 44.9 reduce-scatter.4
  214.8 57.5 all-reduce.3
where the time goes:
time: 284 us; the launch traced here: 283 us
  blocking collectives  161 us (57%)
  waiting for transfers between devices  60.6 us (21%)
  matrix products  23.1 us (8%)
  between operations  15.9 us (6%)
  other arithmetic  12.9 us (5%)
  local copies, waits for them, and re-layouts  6.21 us (2%)
  starting transfers between devices  3.58 us (1%)
    psum x1, blocking collectives, per_device(): lax.psum((loss_part, scale_part), ('dp', 'branch'))  38.5 us
    reduce_scatter x1, waiting for transfers between devices, per_device(): lax.psum_scatter(normalized_exponent_divisor * lax.dot_general(reduced_wi...  25.9 us
    all_gather x1, blocking collectives, per_device(): lax.all_gather(text_down, 'branch', axis=0, tiled=True)  19.6 us
    psum x2, blocking collectives, per_device(): lax.psum((row_mass * jnp.exp(row_peak - row_highest), positive), 'branch')  19.6 us
    all_gather x1, blocking collectives, per_device(): lax.all_gather(image_down, 'branch', axis=0, tiled=True)  17.9 us
    all_gather x1, blocking collectives, per_device(): group_emb = lax.all_gather(image_emb, 'branch', axis=0, tiled=True)  17.6 us
    psum x1, waiting for transfers between devices, per_device(): lax.psum((image_weight, text_weight), 'dp')  14.1 us
    reduce_scatter x1, waiting for transfers between devices, per_device(): lax.psum_scatter(normalized_exponent_divisor * jnp.dot(reduced_width_para...  14 us
  transfers between devices with their start and end apart: 5, of which 4 were waited for; matrix products, arithmetic and copies ran while one was open for 7% of the time, Pallas kernels for 0%

commit v1 on v0

v1 whole, which is shorter than its diff:
```python
import functools

import jax
import jax.numpy as jnp
from jax import lax
from jax.experimental import pallas as pl
from jax.experimental.pallas import tpu as pltpu
from jax.sharding import PartitionSpec as P

NORM_EPSILON = 1e-06
MESH = pl.DeviceIdType.MESH
VMEM = pltpu.VMEM
BF = jnp.bfloat16
F32 = jnp.float32


def xor(me, r):
    out, bit = me, 1
    while bit <= r:
        if r & bit:
            out = out + bit * (1 - 2 * lax.rem(lax.div(me, bit), 2))
        bit *= 2
    return out


def span(masks):
    held = [0]
    for m in masks:
        held = held + [r ^ m for r in held]
    return held


def orders(count):
    bits = []
    b = 2
    while b < count:
        bits.append(b)
        b *= 2
    return [[1] + bits, [1] + bits[::-1]]


def halves(width):
    return [pl.ds(0, width // 2), pl.ds(width // 2, width - width // 2)]


def send(src, dst, ssem, rsem, axis, peer):
    return pltpu.make_async_remote_copy(
        src_ref=src, dst_ref=dst, send_sem=ssem, recv_sem=rsem, device_id={axis: peer}, device_id_type=MESH
    )


def greet(pairs):
    barrier = pltpu.get_barrier_semaphore()
    for axis, peer in pairs:
        pl.semaphore_signal(barrier, inc=1, device_id={axis: peer}, device_id_type=MESH)
    pl.semaphore_wait(barrier, len(pairs))


class CubeGather:
    def __init__(self, me, count, out, ssem, rsem, absolute):
        self.me, self.count, self.out, self.ssem, self.rsem = me, count, out, ssem, rsem
        self.absolute = absolute
        self.orders = [o[::-1] for o in orders(count)]
        self.cols = halves(out.shape[2])
        self.arriving, self.sent = [{}, {}], []

    def slot(self, r):
        return xor(self.me, r) if self.absolute else r

    def stage(self, i, h):
        m = self.orders[h][i]
        for r in span(self.orders[h][:i]):
            self.ready(h, r)
            c = self.cols[h]
            here = self.slot(r)
            there = here if self.absolute else r ^ m
            cp = send(
                self.out.at[here, :, c], self.out.at[there, :, c], self.ssem.at[h, r ^ m], self.rsem.at[h, r ^ m],
                "dp", xor(self.me, m),
            )
            cp.start()
            self.arriving[h][r ^ m] = cp
            self.sent.append(cp)

    def ready(self, h, r):
        cp = self.arriving[h].pop(r, None)
        if cp is not None:
            cp.wait_recv()

    def steps(self):
        return len(self.orders[0])

    def finish(self):
        for h in (0, 1):
            for r in list(self.arriving[h]):
                self.ready(h, r)
        for cp in self.sent:
            cp.wait_send()


class CubeReduce:
    def __init__(self, me, count, src, acc, rcv, ssem, rsem, absolute):
        self.me, self.count, self.src, self.acc, self.rcv = me, count, src, acc, rcv
        self.ssem, self.rsem, self.absolute = ssem, rsem, absolute
        self.orders = orders(count)
        self.cols = halves(src.shape[2])
        self.live = {}
        self.sent = []

    def steps(self):
        return len(self.orders[0])

    def slot(self, r):
        return xor(self.me, r) if self.absolute else r

    def place(self, h, i, k):
        base = sum(self.count >> (j + 1) for j in range(i))
        return base + sorted(span(self.orders[h][i + 1 :])).index(k)

    def start(self, i, h, r):
        m = self.orders[h][i]
        k = r ^ m
        p = self.place(h, i, k)
        c = self.cols[h]
        src = self.src.at[self.slot(r), :, c] if i == 0 else self.acc.at[r, :, c]
        cp = send(src, self.rcv.at[p, :, c], self.ssem.at[h, p], self.rsem.at[h, p], "dp", xor(self.me, m))
        cp.start()
        self.live[(h, i, k)] = cp
        self.sent.append(cp)

    def first(self):
        for h in (0, 1):
            m = self.orders[h][0]
            for r in span(self.orders[h]):
                if r & m:
                    self.start(0, h, r)

    def merge(self, i, h):
        c = self.cols[h]
        later = self.orders[h][i + 1] if i + 1 < self.steps() else 0
        for k in sorted(span(self.orders[h][i + 1 :]), key=lambda k: 0 if k & later else 1):
            self.live[(h, i, k)].wait_recv()
            mine = self.src[self.slot(k), :, c] if i == 0 else self.acc[k, :, c]
            self.acc[k, :, c] = mine + self.rcv[self.place(h, i, k), :, c]
            if k & later:
                self.start(i + 1, h, k)

    def finish(self):
        for cp in self.sent:
            cp.wait_send()


def project_kernel(n, count, ih, th, ip, tp, gi, gt, iu, il, tu, tl, ib, tb, s1, r1, s2, r2, s3, r3):
    b, d = lax.axis_index("branch"), lax.axis_index("dp")
    masks = orders(count)[0]
    greet([("branch", xor(b, r)) for r in range(1, n)] + [("dp", xor(d, m)) for m in masks])
    copies = []
    for j, (src, dst) in enumerate(((th, tb), (ih, ib))):
        for r in range(1, n):
            p = xor(b, r)
            cp = send(src.at[p], dst.at[r], s1.at[j, r], r1.at[j, r], "branch", p)
            cp.start()
            copies.append((j, r, cp))

    def project(j, src, dst, proj, unit, length, out_slot):
        raw = jnp.dot(src[b], proj[b], preferred_element_type=F32)
        for jj, r, cp in copies:
            if jj == j:
                cp.wait_recv()
                raw = raw + jnp.dot(dst[r], proj[xor(b, r)], preferred_element_type=F32)
        size = jnp.sqrt(jnp.sum(raw * raw, axis=1, keepdims=True) + NORM_EPSILON)
        u = raw / size
        unit[...] = u
        length[...] = jnp.broadcast_to(size, length.shape)
        out_slot[...] = u.astype(BF)

    project(0, th, tb, tp, tu, tl, gt.at[0])
    gather = CubeGather(d, count, gt, s2, r2, False)
    for h in (0, 1):
        gather.stage(0, h)
    project(1, ih, ib, ip, iu, il, gi.at[b])
    mine = []
    for r in range(1, n):
        cp = send(gi.at[b], gi.at[b], s3.at[r], r3.at[r], "branch", xor(b, r))
        cp.start()
        mine.append(cp)
    for i in range(1, gather.steps()):
        for h in (0, 1):
            gather.stage(i, h)
    gather.finish()
    for cp in mine:
        cp.wait()
    for _, _, cp in copies:
        cp.wait_send()


def stats_kernel(n, count, rs, cs, row_out, col_out, rb, cb, s1, r1, s2, r2):
    b, d = lax.axis_index("branch"), lax.axis_index("dp")
    greet([("branch", xor(b, r)) for r in range(1, n)] + [("dp", xor(d, m)) for m in range(1, count)])
    rows, columns = [], []
    for m in range(1, count):
        cp = send(cs, cb.at[m], s2.at[m], r2.at[m], "dp", xor(d, m))
        cp.start()
        columns.append(cp)
    for r in range(1, n):
        cp = send(rs, rb.at[r], s1.at[r], r1.at[r], "branch", xor(b, r))
        cp.start()
        rows.append(cp)
    for cp in rows:
        cp.wait()
    peak = rs[0]
    for r in range(1, n):
        peak = jnp.maximum(peak, rb[r, 0])
    mass = rs[1] * jnp.exp(rs[0] - peak)
    positive = rs[2]
    for r in range(1, n):
        mass = mass + rb[r, 1] * jnp.exp(rb[r, 0] - peak)
        positive = positive + rb[r, 2]
    row_out[0] = peak + jnp.log(mass)
    row_out[1] = positive
    for cp in columns:
        cp.wait()
    for k in range(count):
        peak = cs[0, k]
        for m in range(1, count):
            peak = jnp.maximum(peak, cb[m, 0, k ^ m])
        mass = cs[1, k] * jnp.exp(cs[0, k] - peak)
        for m in range(1, count):
            mass = mass + cb[m, 1, k ^ m] * jnp.exp(cb[m, 0, k ^ m] - peak)
        col_out[k] = peak + jnp.log(mass)


def grads_kernel(
    n, count, ipart, tpart, iu, il, tu, tl, sc, gi, gt, sc_out,
    irb, acc, trb, scb, s1, r1, s2, r2, s3, r3, s4, r4,
):
    b, d = lax.axis_index("branch"), lax.axis_index("dp")
    masks = orders(count)[0]
    greet([("branch", xor(b, r)) for r in range(1, n)] + [("dp", xor(d, m)) for m in masks])
    text = CubeReduce(d, count, tpart, acc, trb, s2, r2, False)
    text.first()
    image, scal = [], []
    for r in range(1, n):
        p = xor(b, r)
        cp = send(ipart.at[p], irb.at[r], s1.at[r], r1.at[r], "branch", p)
        cp.start()
        image.append(cp)
    for r in range(1, n):
        cp = send(sc, scb.at[r], s4.at[r], r4.at[r], "branch", xor(b, r))
        cp.start()
        scal.append(cp)
    for h in (0, 1):
        text.merge(0, h)
    down_copies = []

    def finish_side(j, up, unit, length, out):
        u = unit[...]
        radial = jnp.sum(up * u, axis=1, keepdims=True)
        out[b] = ((up - u * radial) / length[:, 0:1]).astype(BF)
        for r in range(1, n):
            cp = send(out.at[b], out.at[b], s3.at[j, r], r3.at[j, r], "branch", xor(b, r))
            cp.start()
            down_copies.append(cp)

    def image_side():
        up = ipart[b]
        for r in range(1, n):
            image[r - 1].wait_recv()
            up = up + irb[r]
        finish_side(0, up, iu, il, gi)

    for i in range(1, text.steps()):
        if i == text.steps() - 1:
            image_side()
        for h in (0, 1):
            text.merge(i, h)
    if text.steps() == 1:
        image_side()
    finish_side(1, acc[0], tu, tl, gt)
    total = sc[...]
    for r in range(1, n):
        scal[r - 1].wait()
        total = total + scb[r]
    sc_out[...] = total
    text.finish()
    for cp in image:
        cp.wait_send()
    for cp in down_copies:
        cp.wait()


def weight_kernel(n, count, w, sc, out, sc_out, acc, rcv, scb, s1, r1, s2, r2, s3, r3):
    d = lax.axis_index("dp")
    greet([("dp", xor(d, m)) for m in range(1, count)])
    red = CubeReduce(d, count, w, acc, rcv, s1, r1, True)
    red.first()
    scal = []
    for m in range(1, count):
        cp = send(sc, scb.at[m], s3.at[m], r3.at[m], "dp", xor(d, m))
        cp.start()
        scal.append(cp)
    gather = CubeGather(d, count, out, s2, r2, True)
    for i in range(red.steps()):
        for h in (0, 1):
            red.merge(i, h)
            if i == red.steps() - 1:
                c = red.cols[h]
                out[d, :, c] = acc[0, :, c]
                gather.stage(0, h)
    for i in range(1, gather.steps()):
        for h in (0, 1):
            gather.stage(i, h)
    total = sc[...]
    for m in range(1, count):
        scal[m - 1].wait()
        total = total + scb[m]
    sc_out[...] = total
    gather.finish()
    red.finish()


def call(body, outs, scratch, args, cid):
    spec = pl.BlockSpec(memory_space=VMEM)
    return pl.pallas_call(
        body,
        out_shape=[jax.ShapeDtypeStruct(s, t) for s, t in outs],
        in_specs=[spec] * len(args),
        out_specs=[spec] * len(outs),
        scratch_shapes=scratch,
        compiler_params=pltpu.CompilerParams(
            collective_id=cid, has_side_effects=True, vmem_limit_bytes=60 * 1024 * 1024
        ),
    )(*args)


def per_device(image_hidden, text_hidden, image_proj, text_proj, log_inverse_sharpness, partner):
    n = lax.axis_size("branch")
    count = lax.axis_size("dp")
    branch_pos = lax.axis_index("branch")
    data_pos = lax.axis_index("dp")
    group_rows, image_cols = image_hidden.shape
    text_cols = text_hidden.shape[1]
    own = group_rows // n
    embed = image_proj.shape[1]
    total_pairs = group_rows * count
    denominator = 2.0 * total_pairs
    dma = pltpu.SemaphoreType.DMA
    scale = jnp.exp(log_inverse_sharpness[0])

    group_emb, text_emb, iu, il, tu, tl = call(
        functools.partial(project_kernel, n, count),
        [((n, own, embed), BF), ((count, own, embed), BF), ((own, embed), F32), ((own, 128), F32),
         ((own, embed), F32), ((own, 128), F32)],
        [VMEM((n, own, image_cols), BF), VMEM((n, own, text_cols), BF), dma((2, n)), dma((2, n)),
         dma((2, count)), dma((2, count)), dma((n,)), dma((n,))],
        (image_hidden.reshape(n, own, image_cols), text_hidden.reshape(n, own, text_cols),
         image_proj.reshape(n, image_cols, embed), text_proj.reshape(n, text_cols, embed)),
        0,
    )
    group_emb = group_emb.reshape(group_rows, embed)
    text_emb = text_emb.reshape(count * own, embed)

    logits = scale * lax.dot_general(
        group_emb, text_emb, (((1,), (1,)), ((), ())), preferred_element_type=F32
    )
    row_partner = lax.dynamic_slice_in_dim(partner, data_pos * group_rows, group_rows, 0)
    blocks = jnp.bitwise_xor(jnp.arange(count, dtype=jnp.int32), data_pos)
    column_ids = (
        (blocks[:, None] * n + branch_pos) * own + jnp.arange(own, dtype=jnp.int32)[None, :]
    ).reshape(-1)
    matched = row_partner[:, None] == column_ids[None, :]
    positive = jnp.sum(jnp.where(matched, logits, 0.0), axis=1)
    row_peak = jnp.max(logits, axis=1)
    row_mass = jnp.sum(jnp.exp(logits - row_peak[:, None]), axis=1)
    col_peak = jnp.max(logits, axis=0)
    col_mass = jnp.sum(jnp.exp(logits - col_peak[None, :]), axis=0)
    rs = jnp.stack([row_peak, row_mass, positive]).reshape(3, n, own)
    cs = jnp.stack([col_peak, col_mass]).reshape(2, count, 1, own)
    row_stats, col_lse = call(
        functools.partial(stats_kernel, n, count),
        [((2, n, own), F32), ((count, 1, own), F32)],
        [VMEM((n, 3, n, own), F32), VMEM((count, 2, count, 1, own), F32), dma((n,)), dma((n,)),
         dma((count,)), dma((count,))],
        (rs, cs),
        1,
    )
    row_lse, positive = row_stats[0], row_stats[1]
    own_rows = lax.dynamic_slice_in_dim(row_lse - 2.0 * positive, branch_pos, 1, 0)
    loss_part = (jnp.sum(own_rows) + jnp.sum(col_lse[0])) / denominator
    row_lse = row_lse.reshape(-1)
    col_lse = col_lse.reshape(-1)

    weights = (
        jnp.exp(logits - row_lse[:, None])
        + jnp.exp(logits - col_lse[None, :])
        - 2.0 * matched.astype(F32)
    ) / denominator
    scale_part = jnp.sum(weights * logits)
    low = weights.astype(BF)
    ipart = scale * jnp.dot(low, text_emb, preferred_element_type=F32)
    tpart = scale * lax.dot_general(low, group_emb, (((0,), (0,)), ((), ())), preferred_element_type=F32)
    sc = jnp.concatenate([jnp.full((1, 128), loss_part, F32), jnp.full((1, 128), scale_part, F32)])
    gi, gt, sc = call(
        functools.partial(grads_kernel, n, count),
        [((n, own, embed), BF), ((n, own, embed), BF), ((2, 128), F32)],
        [VMEM((n, own, embed), F32), VMEM((count, own, embed), F32), VMEM((count - 1, own, embed), F32),
         VMEM((n, 2, 128), F32), dma((n,)), dma((n,)), dma((2, count)), dma((2, count)),
         dma((2, n)), dma((2, n)), dma((n,)), dma((n,))],
        (ipart.reshape(n, own, embed), tpart.reshape(count, own, embed), iu, il, tu, tl, sc),
        2,
    )
    gi = gi.reshape(group_rows, embed)
    gt = gt.reshape(group_rows, embed)
    image_weight = lax.dot_general(
        image_hidden, gi, (((0,), (0,)), ((), ())), preferred_element_type=F32
    )
    text_weight = lax.dot_general(
        text_hidden, gt, (((0,), (0,)), ((), ())), preferred_element_type=F32
    )
    stacked = jnp.concatenate([image_weight, text_weight]).reshape(
        count, (image_cols + text_cols) // count, embed
    )
    summed, sc = call(
        functools.partial(weight_kernel, n, count),
        [(stacked.shape, F32), ((2, 128), F32)],
        [VMEM(stacked.shape, F32), VMEM((count - 1,) + stacked.shape[1:], F32), VMEM((count, 2, 128), F32),
         dma((2, count)), dma((2, count)), dma((2, count)), dma((2, count)), dma((count,)), dma((count,))],
        (stacked, sc),
        3,
    )
    summed = summed.reshape(image_cols + text_cols, embed)
    image_slab = lax.dynamic_slice_in_dim(image_proj, branch_pos * image_cols, image_cols, 0)
    text_slab = lax.dynamic_slice_in_dim(text_proj, branch_pos * text_cols, text_cols, 0)
    grad_image_hidden = jnp.dot(gi, image_slab.T, preferred_element_type=F32).astype(BF)
    grad_text_hidden = jnp.dot(gt, text_slab.T, preferred_element_type=F32).astype(BF)
    return (
        sc[0, :1],
        sc[1, :1],
        grad_image_hidden,
        grad_text_hidden,
        summed[:image_cols],
        summed[image_cols:],
    )


def solution(mesh):
    placed = (P("dp", "branch"), P("dp", "branch"), P(), P(), P(), P())
    return jax.shard_map(
        per_device,
        mesh=mesh,
        in_specs=placed,
        out_specs=(
            P(),
            P(),
            P("dp", "branch"),
            P("dp", "branch"),
            P("branch", None),
            P("branch", None),
        ),
        check_vma=False,
    )
```

time: 284 us -> 181 us (0.64)
  blocking collectives: 161 us -> 0 us
  Pallas kernels: 0 us -> 145 us
  waiting for transfers between devices: 60.6 us -> 0 us
  between operations: 15.9 us -> 2.73 us
  matrix products: 23.1 us -> 16.6 us
  other arithmetic: 12.9 us -> 7.31 us
  starting transfers between devices: 3.58 us -> 0 us
  local copies, waits for them, and re-layouts: 6.21 us -> 9.07 us
    pallas_call x0 -> x4, Pallas kernels: none -> 145 us  [call(): pl.pallas_call(body, out_shape=[jax.ShapeDtypeStruct(s, t) for s, t in ou...]
    psum x4 -> x0, blocking collectives: 70 us -> none  [the longest x1 38.5 us: per_device(): lax.psum((loss_part, scale_part), ('dp', 'branch'))]
    all_gather x3 -> x0, blocking collectives: 55 us -> none  [the longest x1 19.6 us: per_device(): lax.all_gather(text_down, 'branch', axis=0, tiled=True)]
    reduce_scatter x2 -> x0, waiting for transfers between devices: 39.9 us -> none  [the longest x1 25.9 us: per_device(): lax.psum_scatter(normalized_exponent_divisor * lax.dot_general(reduced_wi...]
    pmax x2 -> x0, blocking collectives: 22.1 us -> none  [the longest x1 11.8 us: per_device(): column_highest = lax.pmax(column_peak, 'dp')]
    psum x1 -> x0, waiting for transfers between devices: 14.1 us -> none  [per_device(): lax.psum((image_weight, text_weight), 'dp')]
    all_to_all x1 -> x0, blocking collectives: 13.6 us -> none  [per_device(): lax.all_to_all(text_hidden, 'branch', split_axis=0, concat_axis=1, tiled=...]
    all_to_all x1 -> x0, waiting for transfers between devices: 6.61 us -> none  [per_device(): lax.all_to_all(image_hidden, 'branch', split_axis=0, concat_axis=1, tiled...]
  transfers between devices with their start and end apart: 5 -> 0, of which waited for: 4 -> 0; matrix products, arithmetic and copies ran while one was open for 7% -> 0% of each run, Pallas kernels for 0% -> 0%
where the time goes in v1:
time: 181 us; the launch traced here: 180 us
  Pallas kernels  145 us (80%)
  matrix products  16.6 us (9%)
  local copies, waits for them, and re-layouts  9.07 us (5%)
  other arithmetic  7.31 us (4%)
  between operations  2.73 us (2%)
    pallas_call x4, Pallas kernels, call(): pl.pallas_call(body, out_shape=[jax.ShapeDtypeStruct(s, t) for s, t in ou...  145 us
    dot_general x1, matrix products, per_device(): ipart = scale * jnp.dot(low, text_emb, preferred_element_type=F32)  4.21 us

profile of v1, /device:TPU:0, one launch (start us, length us, event | category | flops | bytes accessed | tf_op | source)
XLA Modules:
  0.0 180.3 jit_solution(16709800984459725763)
XLA Ops:
  1.3 0.8 dynamic_slice.12
  2.1 0.1 add_bitcast_fusion
  2.2 1.8 copy.12
  3.9 36.6 %shard_map.109 = (bf16[4,128,768]{2,1,0:T(8,128)(2,1)}, bf16[8,128,768]{2,1,0:T(8,128)(2,1)}, f32[128,768]{1,0:T(8,128)}, f32[128,128]{1,0:T(8,128)}, f32[128,768]{1,0:T(8,128)}, /*index=5*/f32[128,128]{1,0:T(8,128)}) custom-call(bf16[4,128,256]{2,1,0:T(8,128)(2,1)} %bitcast.51, bf16[4,128,192]{2,1,0:T(8,128)(2,1)} %bitcast.52, ...), custom_call_target="tpu_custom_call" | custom-call | tf_op jit(solution)/shard_map/pallas_call | solution.py:324
  40.6 2.8 %fusion.11 = (f32[1024]{0:T(1024)S(1)}, f32[512]{0:T(512)S(1)}, f32[512,1024]{1,0:T(8,128)S(1)}) fusion(bf16[512,768]{1,0:T(8,128)(2,1)} %bitcast.63, bf16[1024,768]{1,0:T(8,128)(2,1)} %bitcast.61, f32[]{:T(128)} %bitcast), kind=kOutput, calls=%fused_computation.30 | convolution fusion | flops 806877696 | bytes 4462596 | tf_op jit(solution)/shard_map/dot_general | solution.py:363
  43.3 1.0 exponential_reduce_fusion
  44.3 0.6 pad_maximum_fusion.1.cs
  44.9 0.6 pad_maximum_fusion.2.rs
  45.5 9.5 %shard_map.110 = (f32[2,4,128]{2,1,0:T(4,128)}, f32[8,1,128]{2,1,0:T(1,128)}) custom-call(f32[3,4,128]{2,1,0:T(4,128)} %pad_maximum_fusion.2.rs, f32[2,8,1,128]{3,2,1,0:T(1,128)} %pad_maximum_fusion.1.cs), custom_call_target="tpu_custom_call" | custom-call | tf_op jit(solution)/shard_map/pallas_call | solution.py:324
  55.0 0.0 copy-start.3
  55.0 0.7 multiply_subtract_fusion
  55.7 2.6 %multiply_reduce_fusion = f32[]{:T(128)} fusion(f32[512,1024]{1,0:T(8,128)S(1)} %get-tuple-element.41, f32[1024]{0:T(1024)} %bitcast.58, f32[512]{0:T(512)S(1)} %get-tuple-element.38, s32[1024]{0:T(1024)S(1)} %add_bitcast_fusion, s32[512]{0:T(512)S(1)} %dynamic_slice.12), kind=kLoop, calls=%fused_computation.5 | loop fusion | flops 4718591 | bytes 2109444 | tf_op jit(solution)/shard_map/reduce_sum | solution.py:398
  58.3 0.0 copy-done.3
  58.3 0.6 fusion.8
  60.2 0.7 concatenate.10
  60.8 0.0 copy-start.4
  60.8 4.2 %convolution_multiply_fusion.2 = f32[512,768]{1,0:T(8,128)} fusion(bf16[1024,768]{1,0:T(8,128)(2,1)} %bitcast.62, f32[]{:T(128)} %bitcast, f32[512,1024]{1,0:T(8,128)S(1)} %get-tuple-element.41, f32[1024]{0:T(1024)S(1)} %bitcast.59, f32[512]{0:T(512)S(1)} %get-tuple-element.38, s32[1024]{0:T(1024)S(1)} %add_bitcast_fusion, s32[512]{0:T(512)S(1)} %dynamic_slice.12), kind=kOutput, calls=%fused_computation.11 | convolution fusion | flops 809893888 | bytes 5255172 | tf_op jit(solution)/shard_map/dot_general | solution.py:400
  65.1 0.6 concatenate.11.sc
  65.7 0.0 copy-done.4
  65.7 3.3 %convolution_multiply_fusion = f32[1024,768]{1,0:T(8,128)} fusion(bf16[512,768]{1,0:T(8,128)(2,1)S(1)} %bitcast.64, f32[]{:T(128)} %bitcast, f32[512,1024]{1,0:T(8,128)S(1)} %get-tuple-element.41, f32[1024]{0:T(1024)S(1)} %bitcast.60, f32[512]{0:T(512)S(1)} %get-tuple-element.38, s32[1024]{0:T(1024)S(1)} %add_bitcast_fusion, s32[512]{0:T(512)S(1)} %dynamic_slice.12), kind=kOutput, calls=%fused_computation.9 | convolution fusion | flops 810287104 | bytes 6041604 | tf_op jit(solution)/shard_map/dot_general | solution.py:401
  69.0 0.0 copy-start.2
  69.0 74.3 %shard_map.111 = (bf16[4,128,768]{2,1,0:T(8,128)(2,1)}, bf16[4,128,768]{2,1,0:T(8,128)(2,1)}, f32[2,128]{1,0:T(2,128)}) custom-call(f32[4,128,768]{2,1,0:T(8,128)} %bitcast.48, f32[8,128,768]{2,1,0:T(8,128)} %bitcast.41, f32[128,768]{1,0:T(8,128)} %get-tuple-element.23.iu, f32[128,128]{1,0:T(8,128)} %get-tuple-element.24.il, ...), custom_call_target="tpu_custom_call" | custom-call | tf_op jit(solution)/shard_map/pallas_call | solution.py:324
  143.3 0.0 copy-start
  143.3 0.0 copy-start.1
  143.3 2.4 %convolution_convert_fusion.1 = bf16[512,192]{0,1:T(8,128)(2,1)} fusion(bf16[512,768]{1,0:T(8,128)(2,1)} %bitcast.44, bf16[768,768]{1,0:T(8,128)(2,1)} %param.9, s32[]{:T(128)S(6)} %select_n.20), kind=kOutput, calls=%fused_computation.16 | convolution fusion | flops 151093248 | bytes 1277956 | tf_op jit(solution)/shard_map/dot_general | solution.py:435
  145.7 0.0 copy-done.2
  145.7 1.5 convolution_bitcast_fusion.1
  147.2 0.0 copy-done
  147.2 2.1 %convolution_convert_fusion = bf16[512,256]{1,0:T(8,128)(2,1)} fusion(bf16[512,768]{1,0:T(8,128)(2,1)S(1)} %bitcast.42, bf16[1024,768]{1,0:T(8,128)(2,1)} %param.8, s32[]{:T(128)S(6)} %select_n.19), kind=kOutput, calls=%fused_computation.15 | convolution fusion | flops 201457664 | bytes 1441796 | tf_op jit(solution)/shard_map/dot_general | solution.py:434
  149.3 0.0 copy-done.1
  149.3 0.4 convolution_bitcast_fusion
  149.7 1.2 pad_maximum_fusion
  150.9 24.2 %shard_map.112 = (f32[8,56,768]{2,1,0:T(8,128)}, f32[2,128]{1,0:T(2,128)}) custom-call(f32[8,56,768]{2,1,0:T(8,128)} %bitcast.40, f32[2,128]{1,0:T(2,128)} %get-tuple-element.29.sc), custom_call_target="tpu_custom_call" | custom-call | tf_op jit(solution)/shard_map/pallas_call | solution.py:324
  175.1 1.3 fusion.12
  176.3 1.9 %slice.29 = f32[192,768]{1,0:T(8,128)} slice(f32[448,768]{1,0:T(8,128)} %bitcast.49), slice={[256:448], [0:768]} | slice | bytes 1179648 | tf_op jit(solution)/shard_map/slice | solution.py:442
  178.2 2.1 %slice.28 = f32[256,768]{1,0:T(8,128)} slice(f32[448,768]{1,0:T(8,128)} %bitcast.50), slice={[0:256], [0:768]} | slice | bytes 1572864 | tf_op jit(solution)/shard_map/slice | solution.py:441
  (1 shorter events, 0.0 us)
Async XLA Ops:
  55.0 3.3 %copy-start.3 = (f32[8,1,128]{2,1,0:T(1,128)S(1)}, f32[8,1,128]{2,1,0:T(1,128)}, u32[]{:S(2)}) copy-start(f32[8,1,128]{2,1,0:T(1,128)} %get-tuple-element.22) | copy-start | bytes 12292
  60.8 4.9 %copy-start.4 = (bf16[4,128,768]{2,1,0:T(8,128)(2,1)S(1)}, bf16[4,128,768]{2,1,0:T(8,128)(2,1)}, u32[]{:S(2)}) copy-start(bf16[4,128,768]{2,1,0:T(8,128)(2,1)} %get-tuple-element.19) | copy-start | bytes 2359300
  69.0 76.7 %copy-start.2 = (bf16[512,192]{0,1:T(8,128)(2,1)S(1)}, bf16[512,192]{0,1:T(8,128)(2,1)}, u32[]{:S(2)}) copy-start(bf16[512,192]{0,1:T(8,128)(2,1)} %param.7) | copy-start | bytes 589828
  143.3 3.9 %copy-start = (bf16[4,128,768]{2,1,0:T(8,128)(2,1)S(1)}, bf16[4,128,768]{2,1,0:T(8,128)(2,1)}, u32[]{:S(2)}) copy-start(bf16[4,128,768]{2,1,0:T(8,128)(2,1)} %get-tuple-element.27) | copy-start | bytes 2359300
  143.3 6.0 %copy-start.1 = (bf16[512,256]{1,0:T(8,128)(2,1)S(1)}, bf16[512,256]{1,0:T(8,128)(2,1)}, u32[]{:S(2)}) copy-start(bf16[512,256]{1,0:T(8,128)(2,1)} %param.6) | copy-start | bytes 786436

commit v2 on v1

--- a/solution.py
+++ b/solution.py
@@ -56,31 +56,43 @@
     pl.semaphore_wait(barrier, len(pairs))
 
 
+def far_first(count):
+    bits = [1 << k for k in range(count.bit_length() - 1)][::-1]
+    return [bits, bits]
+
+
 class CubeGather:
-    def __init__(self, me, count, out, ssem, rsem, absolute):
-        self.me, self.count, self.out, self.ssem, self.rsem = me, count, out, ssem, rsem
+    def __init__(self, axis, me, masks, out, ssem, rsem, absolute):
+        self.axis, self.me, self.orders, self.out, self.ssem, self.rsem = axis, me, masks, out, ssem, rsem
         self.absolute = absolute
-        self.orders = [o[::-1] for o in orders(count)]
         self.cols = halves(out.shape[2])
         self.arriving, self.sent = [{}, {}], []
 
     def slot(self, r):
         return xor(self.me, r) if self.absolute else r
 
-    def stage(self, i, h):
+    def push(self, i, h, r):
         m = self.orders[h][i]
-        for r in span(self.orders[h][:i]):
-            self.ready(h, r)
-            c = self.cols[h]
-            here = self.slot(r)
-            there = here if self.absolute else r ^ m
-            cp = send(
-                self.out.at[here, :, c], self.out.at[there, :, c], self.ssem.at[h, r ^ m], self.rsem.at[h, r ^ m],
-                "dp", xor(self.me, m),
-            )
-            cp.start()
-            self.arriving[h][r ^ m] = cp
-            self.sent.append(cp)
+        self.ready(h, r)
+        c = self.cols[h]
+        here = self.slot(r)
+        there = here if self.absolute else r ^ m
+        cp = send(
+            self.out.at[here, :, c], self.out.at[there, :, c], self.ssem.at[h, r ^ m], self.rsem.at[h, r ^ m],
+            self.axis, xor(self.me, m),
+        )
+        cp.start()
+        self.arriving[h][r ^ m] = cp
+        self.sent.append(cp)
+
+    def own(self, h):
+        for i in range(self.steps()):
+            self.push(i, h, 0)
+
+    def forward(self, i):
+        for h in (0, 1):
+            for r in span(self.orders[h][:i])[1:]:
+                self.push(i, h, r)
 
     def ready(self, h, r):
         cp = self.arriving[h].pop(r, None)
@@ -98,11 +110,19 @@
             cp.wait_send()
 
 
+def dp_gather(me, count, out, ssem, rsem, absolute):
+    return CubeGather("dp", me, [o[::-1] for o in orders(count)], out, ssem, rsem, absolute)
+
+
+def branch_gather(me, n, out, ssem, rsem):
+    return CubeGather("branch", me, far_first(n), out, ssem, rsem, True)
+
+
 class CubeReduce:
-    def __init__(self, me, count, src, acc, rcv, ssem, rsem, absolute):
+    def __init__(self, axis, masks, me, count, src, acc, rcv, ssem, rsem, absolute):
+        self.axis, self.orders = axis, masks
         self.me, self.count, self.src, self.acc, self.rcv = me, count, src, acc, rcv
         self.ssem, self.rsem, self.absolute = ssem, rsem, absolute
-        self.orders = orders(count)
         self.cols = halves(src.shape[2])
         self.live = {}
         self.sent = []
@@ -123,7 +143,7 @@
         p = self.place(h, i, k)
         c = self.cols[h]
         src = self.src.at[self.slot(r), :, c] if i == 0 else self.acc.at[r, :, c]
-        cp = send(src, self.rcv.at[p, :, c], self.ssem.at[h, p], self.rsem.at[h, p], "dp", xor(self.me, m))
+        cp = send(src, self.rcv.at[p, :, c], self.ssem.at[h, p], self.rsem.at[h, p], self.axis, xor(self.me, m))
         cp.start()
         self.live[(h, i, k)] = cp
         self.sent.append(cp)
@@ -175,21 +195,20 @@
         out_slot[...] = u.astype(BF)
 
     project(0, th, tb, tp, tu, tl, gt.at[0])
-    gather = CubeGather(d, count, gt, s2, r2, False)
+    gather = dp_gather(d, count, gt, s2, r2, False)
+    line = branch_gather(b, n, gi, s3, r3)
     for h in (0, 1):
-        gather.stage(0, h)
+        gather.own(h)
     project(1, ih, ib, ip, iu, il, gi.at[b])
-    mine = []
-    for r in range(1, n):
-        cp = send(gi.at[b], gi.at[b], s3.at[r], r3.at[r], "branch", xor(b, r))
-        cp.start()
-        mine.append(cp)
-    for i in range(1, gather.steps()):
-        for h in (0, 1):
-            gather.stage(i, h)
+    for h in (0, 1):
+        line.own(h)
+    for i in range(1, max(gather.steps(), line.steps())):
+        if i < gather.steps():
+            gather.forward(i)
+        if i < line.steps():
+            line.forward(i)
     gather.finish()
-    for cp in mine:
-        cp.wait()
+    line.finish()
     for _, _, cp in copies:
         cp.wait_send()
 
@@ -232,91 +251,87 @@
 
 def grads_kernel(
     n, count, ipart, tpart, iu, il, tu, tl, sc, gi, gt, sc_out,
-    irb, acc, trb, scb, s1, r1, s2, r2, s3, r3, s4, r4,
+    iacc, irb, acc, trb, scb, s1, r1, s2, r2, s3, r3, s4, r4, s5, r5,
 ):
     b, d = lax.axis_index("branch"), lax.axis_index("dp")
     masks = orders(count)[0]
     greet([("branch", xor(b, r)) for r in range(1, n)] + [("dp", xor(d, m)) for m in masks])
-    text = CubeReduce(d, count, tpart, acc, trb, s2, r2, False)
+    text = CubeReduce("dp", orders(count), d, count, tpart, acc, trb, s2, r2, False)
     text.first()
-    image, scal = [], []
-    for r in range(1, n):
-        p = xor(b, r)
-        cp = send(ipart.at[p], irb.at[r], s1.at[r], r1.at[r], "branch", p)
-        cp.start()
-        image.append(cp)
+    near = [o[::-1] for o in far_first(n)]
+    image = CubeReduce("branch", near, b, n, ipart, iacc, irb, s1, r1, True)
+    image.first()
+    scal = []
     for r in range(1, n):
         cp = send(sc, scb.at[r], s4.at[r], r4.at[r], "branch", xor(b, r))
         cp.start()
         scal.append(cp)
-    for h in (0, 1):
-        text.merge(0, h)
-    down_copies = []
-
-    def finish_side(j, up, unit, length, out):
+    image_line = branch_gather(b, n, gi, s3, r3)
+    text_line = branch_gather(b, n, gt, s5, r5)
+
+    def finish_side(line, up, unit, length, out):
         u = unit[...]
         radial = jnp.sum(up * u, axis=1, keepdims=True)
         out[b] = ((up - u * radial) / length[:, 0:1]).astype(BF)
-        for r in range(1, n):
-            cp = send(out.at[b], out.at[b], s3.at[j, r], r3.at[j, r], "branch", xor(b, r))
-            cp.start()
-            down_copies.append(cp)
-
-    def image_side():
-        up = ipart[b]
-        for r in range(1, n):
-            image[r - 1].wait_recv()
-            up = up + irb[r]
-        finish_side(0, up, iu, il, gi)
-
-    for i in range(1, text.steps()):
-        if i == text.steps() - 1:
-            image_side()
+        for h in (0, 1):
+            line.own(h)
+
+    for i in range(text.steps()):
         for h in (0, 1):
             text.merge(i, h)
-    if text.steps() == 1:
-        image_side()
-    finish_side(1, acc[0], tu, tl, gt)
+    for i in range(image.steps()):
+        for h in (0, 1):
+            image.merge(i, h)
+        if i == 0:
+            finish_side(text_line, acc[0], tu, tl, gt)
+    finish_side(image_line, iacc[0], iu, il, gi)
+    for line in (text_line, image_line):
+        for i in range(1, line.steps()):
+            line.forward(i)
     total = sc[...]
     for r in range(1, n):
         scal[r - 1].wait()
         total = total + scb[r]
     sc_out[...] = total
     text.finish()
-    for cp in image:
-        cp.wait_send()
-    for cp in down_copies:
-        cp.wait()
-
-
-def weight_kernel(n, count, w, sc, out, sc_out, acc, rcv, scb, s1, r1, s2, r2, s3, r3):
+    image.finish()
+    image_line.finish()
+    text_line.finish()
+
+
+def weight_kernel(n, count, wi, wt, sc, oi, ot, sc_out, ai, at, ri, rt, scb, s1, r1, s2, r2, s3, r3, s4, r4, s5, r5):
     d = lax.axis_index("dp")
     greet([("dp", xor(d, m)) for m in range(1, count)])
-    red = CubeReduce(d, count, w, acc, rcv, s1, r1, True)
-    red.first()
+    reds = [
+        CubeReduce("dp", orders(count), d, count, wi, ai, ri, s1, r1, True),
+        CubeReduce("dp", orders(count), d, count, wt, at, rt, s4, r4, True),
+    ]
+    for red in reds:
+        red.first()
     scal = []
     for m in range(1, count):
         cp = send(sc, scb.at[m], s3.at[m], r3.at[m], "dp", xor(d, m))
         cp.start()
         scal.append(cp)
-    gather = CubeGather(d, count, out, s2, r2, True)
-    for i in range(red.steps()):
-        for h in (0, 1):
-            red.merge(i, h)
-            if i == red.steps() - 1:
-                c = red.cols[h]
-                out[d, :, c] = acc[0, :, c]
-                gather.stage(0, h)
-    for i in range(1, gather.steps()):
-        for h in (0, 1):
-            gather.stage(i, h)
+    gathers = [dp_gather(d, count, oi, s2, r2, True), dp_gather(d, count, ot, s5, r5, True)]
+    for i in range(reds[0].steps()):
+        for red, gather in zip(reds, gathers):
+            for h in (0, 1):
+                red.merge(i, h)
+                if i == red.steps() - 1:
+                    c = red.cols[h]
+                    gather.out[d, :, c] = red.acc[0, :, c]
+                    gather.own(h)
+    for i in range(1, gathers[0].steps()):
+        for gather in gathers:
+            gather.forward(i)
     total = sc[...]
     for m in range(1, count):
         scal[m - 1].wait()
         total = total + scb[m]
     sc_out[...] = total
-    gather.finish()
-    red.finish()
+    for part in gathers + reds:
+        part.finish()
 
 
 def call(body, outs, scratch, args, cid):
@@ -352,7 +367,7 @@
         [((n, own, embed), BF), ((count, own, embed), BF), ((own, embed), F32), ((own, 128), F32),
          ((own, embed), F32), ((own, 128), F32)],
         [VMEM((n, own, image_cols), BF), VMEM((n, own, text_cols), BF), dma((2, n)), dma((2, n)),
-         dma((2, count)), dma((2, count)), dma((n,)), dma((n,))],
+         dma((2, count)), dma((2, count)), dma((2, n)), dma((2, n))],
         (image_hidden.reshape(n, own, image_cols), text_hidden.reshape(n, own, text_cols),
          image_proj.reshape(n, image_cols, embed), text_proj.reshape(n, text_cols, embed)),
         0,
@@ -403,9 +418,9 @@
     gi, gt, sc = call(
         functools.partial(grads_kernel, n, count),
         [((n, own, embed), BF), ((n, own, embed), BF), ((2, 128), F32)],
-        [VMEM((n, own, embed), F32), VMEM((count, own, embed), F32), VMEM((count - 1, own, embed), F32),
-         VMEM((n, 2, 128), F32), dma((n,)), dma((n,)), dma((2, count)), dma((2, count)),
-         dma((2, n)), dma((2, n)), dma((n,)), dma((n,))],
+        [VMEM((n, own, embed), F32), VMEM((n - 1, own, embed), F32), VMEM((count, own, embed), F32), VMEM((count - 1, own, embed), F32),
+         VMEM((n, 2, 128), F32), dma((2, n)), dma((2, n)), dma((2, count)), dma((2, count)),
+         dma((2, n)), dma((2, n)), dma((n,)), dma((n,)), dma((2, n)), dma((2, n))],
         (ipart.reshape(n, own, embed), tpart.reshape(count, own, embed), iu, il, tu, tl, sc),
         2,
     )
@@ -417,18 +432,18 @@
     text_weight = lax.dot_general(
         text_hidden, gt, (((0,), (0,)), ((), ())), preferred_element_type=F32
     )
-    stacked = jnp.concatenate([image_weight, text_weight]).reshape(
-        count, (image_cols + text_cols) // count, embed
-    )
-    summed, sc = call(
+    image_weight = image_weight.reshape(count, image_cols // count, embed)
+    text_weight = text_weight.reshape(count, text_cols // count, embed)
+    image_sum, text_sum, sc = call(
         functools.partial(weight_kernel, n, count),
-        [(stacked.shape, F32), ((2, 128), F32)],
-        [VMEM(stacked.shape, F32), VMEM((count - 1,) + stacked.shape[1:], F32), VMEM((count, 2, 128), F32),
-         dma((2, count)), dma((2, count)), dma((2, count)), dma((2, count)), dma((count,)), dma((count,))],
-        (stacked, sc),
+        [(image_weight.shape, F32), (text_weight.shape, F32), ((2, 128), F32)],
+        [VMEM(image_weight.shape, F32), VMEM(text_weight.shape, F32),
+         VMEM((count - 1,) + image_weight.shape[1:], F32), VMEM((count - 1,) + text_weight.shape[1:], F32),
+         VMEM((count, 2, 128), F32), dma((2, count)), dma((2, count)), dma((2, count)), dma((2, count)),
+         dma((count,)), dma((count,)), dma((2, count)), dma((2, count)), dma((2, count)), dma((2, count))],
+        (image_weight, text_weight, sc),
         3,
     )
-    summed = summed.reshape(image_cols + text_cols, embed)
     image_slab = lax.dynamic_slice_in_dim(image_proj, branch_pos * image_cols, image_cols, 0)
     text_slab = lax.dynamic_slice_in_dim(text_proj, branch_pos * text_cols, text_cols, 0)
     grad_image_hidden = jnp.dot(gi, image_slab.T, preferred_element_type=F32).astype(BF)
@@ -438,8 +453,8 @@
         sc[1, :1],
         grad_image_hidden,
         grad_text_hidden,
-        summed[:image_cols],
-        summed[image_cols:],
+        image_sum.reshape(image_cols, embed),
+        text_sum.reshape(text_cols, embed),
     )
 
 

time: 181 us -> 169 us (0.934)
  Pallas kernels: 145 us -> 132 us
    pallas_call x4, Pallas kernels: 145 us -> 132 us  [call(): pl.pallas_call(body, out_shape=[jax.ShapeDtypeStruct(s, t) for s, t in ou...]
    unnamed x11 -> x13, local copies, waits for them, and re-layouts: 1.79 us -> 5.77 us
    slice x2 -> x0, local copies, waits for them, and re-layouts: 3.98 us -> none  [the longest x1 2.06 us: per_device(): summed[:image_cols]]
where the time goes in v2:
time: 169 us; the launch traced here: 168 us
  Pallas kernels  132 us (78%)
  matrix products  18.3 us (11%)
  local copies, waits for them, and re-layouts  9.07 us (5%)
  other arithmetic  6.14 us (4%)
  between operations  2.71 us (2%)
    pallas_call x4, Pallas kernels, call(): pl.pallas_call(body, out_shape=[jax.ShapeDtypeStruct(s, t) for s, t in ou...  132 us
    unnamed x13, local copies, waits for them, and re-layouts  5.77 us
    dot_general x1, matrix products, per_device(): ipart = scale * jnp.dot(low, text_emb, preferred_element_type=F32)  4.21 us

profile of v2, /device:TPU:0, one launch (start us, length us, event | category | flops | bytes accessed | tf_op | source)
XLA Modules:
  0.0 168.3 jit_solution(3190244160210808496)
XLA Ops:
  1.3 0.8 dynamic_slice.12
  2.1 0.1 add_bitcast_fusion
  2.2 1.8 %copy.12 = bf16[512,192]{1,0:T(8,128)(2,1)} copy(bf16[512,192]{0,1:T(8,128)(2,1)} %param.7) | data formatting | bytes 393216 | tf_op args[1]
  3.9 34.6 %shard_map.109 = (bf16[4,128,768]{2,1,0:T(8,128)(2,1)}, bf16[8,128,768]{2,1,0:T(8,128)(2,1)}, f32[128,768]{1,0:T(8,128)}, f32[128,128]{1,0:T(8,128)}, f32[128,768]{1,0:T(8,128)}, /*index=5*/f32[128,128]{1,0:T(8,128)}) custom-call(bf16[4,128,256]{2,1,0:T(8,128)(2,1)} %bitcast.52, bf16[4,128,192]{2,1,0:T(8,128)(2,1)} %bitcast.53, ...), custom_call_target="tpu_custom_call" | custom-call | tf_op jit(solution)/shard_map/pallas_call | solution.py:339
  38.5 2.8 %fusion.11 = (f32[1024]{0:T(1024)S(1)}, f32[512]{0:T(512)S(1)}, f32[512,1024]{1,0:T(8,128)S(1)}) fusion(bf16[512,768]{1,0:T(8,128)(2,1)} %bitcast.66, bf16[1024,768]{1,0:T(8,128)(2,1)} %bitcast.64, f32[]{:T(128)} %bitcast), kind=kOutput, calls=%fused_computation.27 | convolution fusion | flops 806877696 | bytes 4462596 | tf_op jit(solution)/shard_map/dot_general | solution.py:378
  41.3 1.0 exponential_reduce_fusion
  42.3 0.6 pad_maximum_fusion.cs
  42.9 0.6 pad_maximum_fusion.1.rs
  43.5 8.2 %shard_map.110 = (f32[2,4,128]{2,1,0:T(4,128)}, f32[8,1,128]{2,1,0:T(1,128)}) custom-call(f32[3,4,128]{2,1,0:T(4,128)} %pad_maximum_fusion.1.rs, f32[2,8,1,128]{3,2,1,0:T(1,128)} %pad_maximum_fusion.cs), custom_call_target="tpu_custom_call" | custom-call | tf_op jit(solution)/shard_map/pallas_call | solution.py:339
  51.7 0.0 copy-start.3
  51.7 0.7 multiply_subtract_fusion
  52.4 2.6 %multiply_reduce_fusion = f32[]{:T(128)} fusion(f32[512,1024]{1,0:T(8,128)S(1)} %get-tuple-element.43, f32[1024]{0:T(1024)} %bitcast.61, f32[512]{0:T(512)S(1)} %get-tuple-element.40, s32[1024]{0:T(1024)S(1)} %add_bitcast_fusion, s32[512]{0:T(512)S(1)} %dynamic_slice.12), kind=kLoop, calls=%fused_computation.5 | loop fusion | flops 4718591 | bytes 2109444 | tf_op jit(solution)/shard_map/reduce_sum | solution.py:413
  54.9 0.0 copy-done.3
  54.9 0.6 fusion.8
  56.9 0.7 concatenate.7
  57.5 0.0 copy-start.4
  57.5 4.2 %convolution_multiply_fusion.2 = f32[512,768]{1,0:T(8,128)} fusion(bf16[1024,768]{1,0:T(8,128)(2,1)} %bitcast.65, f32[]{:T(128)} %bitcast, f32[512,1024]{1,0:T(8,128)S(1)} %get-tuple-element.43, f32[1024]{0:T(1024)S(1)} %bitcast.62, f32[512]{0:T(512)S(1)} %get-tuple-element.40, s32[1024]{0:T(1024)S(1)} %add_bitcast_fusion, s32[512]{0:T(512)S(1)} %dynamic_slice.12), kind=kOutput, calls=%fused_computation.11 | convolution fusion | flops 809893888 | bytes 5255172 | tf_op jit(solution)/shard_map/dot_general | solution.py:415
  61.7 0.6 concatenate.8.sc
  62.4 0.0 copy-done.4
  62.4 3.3 %convolution_multiply_fusion = f32[1024,768]{1,0:T(8,128)} fusion(bf16[512,768]{1,0:T(8,128)(2,1)S(1)} %bitcast.67, f32[]{:T(128)} %bitcast, f32[512,1024]{1,0:T(8,128)S(1)} %get-tuple-element.43, f32[1024]{0:T(1024)S(1)} %bitcast.63, f32[512]{0:T(512)S(1)} %get-tuple-element.40, s32[1024]{0:T(1024)S(1)} %add_bitcast_fusion, s32[512]{0:T(512)S(1)} %dynamic_slice.12), kind=kOutput, calls=%fused_computation.9 | convolution fusion | flops 810287104 | bytes 6041604 | tf_op jit(solution)/shard_map/dot_general | solution.py:416
  65.6 0.0 copy-start.2
  65.6 65.4 %shard_map.111 = (bf16[4,128,768]{2,1,0:T(8,128)(2,1)}, bf16[4,128,768]{2,1,0:T(8,128)(2,1)}, f32[2,128]{1,0:T(2,128)}) custom-call(f32[4,128,768]{2,1,0:T(8,128)} %bitcast.51, f32[8,128,768]{2,1,0:T(8,128)} %bitcast.43, f32[128,768]{1,0:T(8,128)} %get-tuple-element.24.iu, f32[128,128]{1,0:T(8,128)} %get-tuple-element.25.il, ...), custom_call_target="tpu_custom_call" | custom-call | tf_op jit(solution)/shard_map/pallas_call | solution.py:339
  131.1 0.0 copy-start
  131.1 0.0 copy-start.1
  131.1 2.4 %convolution_convert_fusion.1 = bf16[512,192]{0,1:T(8,128)(2,1)} fusion(bf16[512,768]{1,0:T(8,128)(2,1)} %bitcast.46, bf16[768,768]{1,0:T(8,128)(2,1)} %param.9, s32[]{:T(128)S(6)} %select_n.20), kind=kOutput, calls=%fused_computation.13 | convolution fusion | flops 151093248 | bytes 1277956 | tf_op jit(solution)/shard_map/dot_general | solution.py:450
  133.5 0.0 copy-done.2
  133.5 2.3 %fusion.14 = f32[768,192]{0,1:T(8,128)} fusion(bf16[512,192]{0,1:T(8,128)(2,1)S(1)} %copy-done.2, bf16[512,768]{1,0:T(8,128)(2,1)} %bitcast.47), kind=kOutput, calls=%fused_computation.30 | convolution fusion | flops 150994944 | bytes 1572864 | tf_op jit(solution)/shard_map/dot_general | solution.py:432
  135.7 0.0 copy-done
  135.7 2.1 %convolution_convert_fusion = bf16[512,256]{1,0:T(8,128)(2,1)} fusion(bf16[512,768]{1,0:T(8,128)(2,1)S(1)} %bitcast.44, bf16[1024,768]{1,0:T(8,128)(2,1)} %param.8, s32[]{:T(128)S(6)} %select_n.19), kind=kOutput, calls=%fused_computation.12 | convolution fusion | flops 201457664 | bytes 1441796 | tf_op jit(solution)/shard_map/dot_general | solution.py:449
  137.8 0.0 copy-done.1
  137.8 1.3 fusion.13
  139.1 23.9 %shard_map.112 = (f32[8,32,768]{2,1,0:T(8,128)}, f32[8,24,768]{2,1,0:T(8,128)}, f32[2,128]{1,0:T(2,128)}) custom-call(f32[8,32,768]{2,1,0:T(8,128)} %bitcast.42, f32[8,24,768]{2,1,0:T(8,128)} %bitcast.49, f32[2,128]{1,0:T(2,128)} %get-tuple-element.30.sc), custom_call_target="tpu_custom_call" | custom-call | tf_op jit(solution)/shard_map/pallas_call | solution.py:339
  163.1 1.3 fusion.12
  164.3 2.1 %copy.16 = f32[256,768]{1,0:T(8,128)} copy(f32[256,768]{1,0:T(8,128)} %bitcast.54) | data formatting | bytes 1572864
  166.4 1.9 %copy.17 = f32[192,768]{1,0:T(8,128)} copy(f32[192,768]{1,0:T(8,128)} %bitcast.55) | data formatting | bytes 1179648
  (1 shorter events, 0.0 us)
Async XLA Ops:
  51.7 3.3 %copy-start.3 = (f32[8,1,128]{2,1,0:T(1,128)S(1)}, f32[8,1,128]{2,1,0:T(1,128)}, u32[]{:S(2)}) copy-start(f32[8,1,128]{2,1,0:T(1,128)} %get-tuple-element.23) | copy-start | bytes 12292
  57.5 4.9 %copy-start.4 = (bf16[4,128,768]{2,1,0:T(8,128)(2,1)S(1)}, bf16[4,128,768]{2,1,0:T(8,128)(2,1)}, u32[]{:S(2)}) copy-start(bf16[4,128,768]{2,1,0:T(8,128)(2,1)} %get-tuple-element.20) | copy-start | bytes 2359300
  65.6 67.8 %copy-start.2 = (bf16[512,192]{0,1:T(8,128)(2,1)S(1)}, bf16[512,192]{0,1:T(8,128)(2,1)}, u32[]{:S(2)}) copy-start(bf16[512,192]{0,1:T(8,128)(2,1)} %param.7) | copy-start | bytes 589828
  131.1 4.7 %copy-start = (bf16[4,128,768]{2,1,0:T(8,128)(2,1)S(1)}, bf16[4,128,768]{2,1,0:T(8,128)(2,1)}, u32[]{:S(2)}) copy-start(bf16[4,128,768]{2,1,0:T(8,128)(2,1)} %get-tuple-element.28) | copy-start | bytes 2359300
  131.1 6.8 %copy-start.1 = (bf16[512,256]{1,0:T(8,128)(2,1)S(1)}, bf16[512,256]{1,0:T(8,128)(2,1)}, u32[]{:S(2)}) copy-start(bf16[512,256]{1,0:T(8,128)(2,1)} %param.6) | copy-start | bytes 786436
